TPU v7x, 32 devices: a whole 2x2x4 slice. The times are simulated.
32 devices in a mesh: gx: 4 (over y, x), gy: 2 (over core), gz: 4 (over z).
Axes of the slice: x: 2, y: 2, z: 4, core: 2. Of those that a mesh axis runs over, the one named last changes fastest.
Arguments:
- residual_in: float32 [256, 128, 1024], P('gx', 'gy', 'gz'), may hold values from -700 to 700
Outputs:
- level_one: float32 [128, 64, 512], P('gx', 'gy', 'gz')
- level_two: float32 [64, 32, 256], P('gx', 'gy', 'gz')
- level_three: float32 [32, 16, 128], P('gx', 'gy', 'gz')
- level_four: float32 [16, 8, 64], P('gx', 'gy', 'gz')
- level_five: float32 [8, 4, 32], P('gx', 'gy', 'gz')
- level_scales: float32 [5], replicated
All inputs are finite; a program needn't handle non-finite values.
Results may differ from a plain program's by a relative error of at most 0.0002.
Values sent between devices are 32-bit elements; how exact they have to be, the bound alone decides.
A program may use at most 64 MiB of HBM per device.

v0:
```python
import jax
import jax.numpy as jnp
from jax import lax
from jax.sharding import PartitionSpec as P

LEVELS = 5


EPSILON = 1e-06


def shifted(block, axis, distance):
    devices = range(lax.axis_size(axis))
    route = [(i - distance, i) for i in devices if i - distance in devices]
    return lax.ppermute(block, axis, route)


def pass_axis(values, axis_pos, rim_plane):
    length = values.shape[axis_pos]
    half = length // 2
    if axis_pos == 2:
        rows = lax.broadcasted_iota(jnp.int32, (length, half), 0)
        cols = lax.broadcasted_iota(jnp.int32, (length, half), 1)
        table = jnp.where(
            rows == 2 * cols,
            0.5,
            jnp.where((rows == 2 * cols + 1) | (rows == 2 * cols - 1), 0.25, 0.0),
        ).astype(jnp.float32)
        reduced = lax.dot_general(
            values,
            table,
            (((2,), (0,)), ((), ())),
            precision=lax.Precision.HIGHEST,
            preferred_element_type=jnp.float32,
        )
        tail = jnp.zeros(values.shape[:2] + (half - 1,), jnp.float32)
        return reduced + jnp.concatenate([0.25 * rim_plane, tail], axis=2)
    new_shape = values.shape[:axis_pos] + (half, 2) + values.shape[axis_pos + 1 :]
    paired = values.reshape(new_shape)
    even_part = lax.index_in_dim(paired, 0, axis_pos + 1, False)
    odd_part = lax.index_in_dim(paired, 1, axis_pos + 1, False)
    earlier = jnp.concatenate(
        [rim_plane, lax.slice_in_dim(odd_part, 0, half - 1, 1, axis_pos)], axis=axis_pos
    )
    return 0.5 * even_part + 0.25 * odd_part + 0.25 * earlier


def extend_cube(values):
    plane_x = shifted(values[-1:, :, :], "gx", 1)
    values = jnp.concatenate([plane_x, values], axis=0)
    plane_y = shifted(values[:, -1:, :], "gy", 1)
    values = jnp.concatenate([plane_y, values], axis=1)
    plane_z = shifted(values[:, :, -1:], "gz", 1)
    return jnp.concatenate([plane_z, values], axis=2)


def combine_cube(padded):
    values = pass_axis(padded[1:], 0, padded[:1])
    values = pass_axis(values[:, 1:], 1, values[:, :1])
    return pass_axis(values[:, :, 1:], 2, values[:, :, :1])


def restrict_any(values):
    return combine_cube(extend_cube(values))


def per_device(residual_in):
    devices_all = lax.axis_size("gx") * lax.axis_size("gy") * lax.axis_size("gz")
    current = residual_in
    grid_list = []
    scale_list = []
    unscaled = []
    sums_local = []
    for step_no in range(LEVELS):
        coarse = restrict_any(current)
        sums_local.append(jnp.sum(coarse * coarse))
        unscaled.append(coarse)
        current = coarse
    totals = lax.psum(jnp.stack(sums_local), ("gx", "gy", "gz"))
    product = jnp.float32(1.0)
    for step_no in range(LEVELS):
        cells = unscaled[step_no].size * devices_all
        scale_now = jnp.sqrt(totals[step_no] / (product * product) / cells + EPSILON)
        product = product * scale_now
        grid_list.append(unscaled[step_no] / product)
        scale_list.append(scale_now)
    return (
        grid_list[0],
        grid_list[1],
        grid_list[2],
        grid_list[3],
        grid_list[4],
        jnp.stack(scale_list),
    )


def solution(mesh):
    placed = (P("gx", "gy", "gz"),)
    return jax.shard_map(
        per_device,
        mesh=mesh,
        in_specs=placed,
        out_specs=(
            P("gx", "gy", "gz"),
            P("gx", "gy", "gz"),
            P("gx", "gy", "gz"),
            P("gx", "gy", "gz"),
            P("gx", "gy", "gz"),
            P(),
        ),
        check_vma=False,
    )
```

profile of v0, /device:TPU:0, one launch (start us, length us, event | category | flops | bytes accessed | tf_op | source)
XLA Modules:
  0.0 157.5 jit_solution(14000450861790597113)
XLA Ops:
  0.6 0.8 slice.260
  1.5 4.9 %collective-permute-start = (f32[1,64,256]{2,1,0:T(8,128)S(1)}, f32[1,64,256]{2,1,0:T(8,128)S(1)}, u32[]{:S(2)}, u32[]{:S(2)}) collective-permute-start(f32[1,64,256]{2,1,0:T(8,128)S(1)} %slice.260), channel_id=1, source_target_pairs={{0,8},{8,16},{16,24},{1,9},{9,17},{17,25},{2,10},{10,18},{18,26},{... | collective-permute-start | bytes 196616 | tf_op jit(solution)/shard_map/ppermute | solution.py:15
  6.3 1.9 %collective-permute-done = f32[1,64,256]{2,1,0:T(8,128)S(1)} collective-permute-done((f32[1,64,256]{2,1,0:T(8,128)S(1)}, f32[1,64,256]{2,1,0:T(8,128)S(1)}, u32[]{:S(2)}, u32[]{:S(2)}) %collective-permute-start) | collective-permute-done | bytes 65568 | tf_op jit(solution)/shard_map/ppermute | solution.py:15
  8.2 3.0 %constant_dynamic-update-slice_fusion = f32[65,64,256]{2,1,0:T(8,128)S(1)} fusion(f32[65,64,256]{2,1,0:T(8,128)S(1)} %constant_dynamic-update-slice_fusion.1, f32[64,64,256]{2,1,0:T(8,128)} %param.1), kind=kLoop, calls=%fused_computation.182 | loop fusion | bytes 8388608 | tf_op jit(solution)/shard_map/concatenate | solution.py:50
  11.3 1.3 collective-permute-start.1
  12.6 0.9 collective-permute-done.1
  13.5 0.8 pad_maximum_fusion
  14.2 0.8 copy.49
  15.1 3.5 %collective-permute-start.2 = (f32[65,65,1]{1,2,0:T(1,128)S(1)}, f32[65,65,1]{1,2,0:T(1,128)S(1)}, u32[]{:S(2)}, u32[]{:S(2)}) collective-permute-start(f32[65,65,1]{1,2,0:T(1,128)S(1)} %copy.49), channel_id=1, source_target_pairs={{0,1},{1,2},{2,3},{4,5},{5,6},{6,7},{8,9},{9,10},{10,11},{12,13},{... | collective-permute-start | bytes 50708 | tf_op jit(solution)/shard_map/ppermute | solution.py:15
  18.6 1.6 collective-permute-done.2
  20.1 0.9 copy.50
  21.1 4.7 %maximum_maximum_fusion = f32[65,65,257]{2,1,0:T(8,128)S(1)} fusion(f32[65,64,256]{2,1,0:T(8,128)} %copy-done, f32[65,1,256]{2,1,0:T(1,128)S(1)} %collective-permute-done.1, f32[65,65,1]{2,1,0:T(8,128)S(1)} %copy.50), kind=kLoop, calls=%fused_computation | loop fusion | flops 2171650 | bytes 8686600 | tf_op jit(solution)/shard_map/concatenate | solution.py:54
  26.6 2.1 %fusion.2 = f32[32,65,257]{2,1,0:T(8,128)S(1)} fusion(f32[65,65,1]{2,1,0:T(8,128)S(1)} %copy.50, f32[65,64,256]{2,1,0:T(8,128)S(1)} %bitcast.209, f32[65,1,256]{2,1,0:T(1,128)S(1)} %collective-permute-done.1, f32[32,2,65,257]{3,2,1,0:T(8,128)S(1)} %bitcast.207, f32[31,65,257]{2,1,0:T(8,128)S(1)} %slice_bitcast_fusion.2), kind=kLoop, calls=%fused_computation.4 | loop fusion | flops 6414720 | bytes 12829440 | tf_op jit(solution)/shard_map/add | solution.py:45
  29.2 1.8 %copy.55 = f32[32,64,257]{2,0,1:T(8,128)S(1)} copy(f32[32,64,257]{2,1,0:T(8,128)S(1)} %slice.350) | data formatting | bytes 4210688 | tf_op jit(solution)/shard_map/slice | solution.py:59
  31.3 0.9 copy.151
  32.2 2.0 %fusion.10 = f32[32,32,257]{2,1,0:T(8,128)S(1)} fusion(f32[32,31,257]{2,1,0:T(8,128)S(1)} %bitcast.213, f32[32,1,257]{2,1,0:T(1,128)S(1)} %slice.353, f32[32,32,1,257]{3,0,2,1:T(8,128)S(1)} %get-tuple-element.6, f32[32,32,1,257]{3,0,2,1:T(8,128)S(1)} %get-tuple-element.7), kind=kLoop, calls=%fused_computation.18 | loop fusion | flops 1579008 | bytes 4210688 | tf_op jit(solution)/shard_map/add | solution.py:45
  34.2 1.6 %multiply_reduce_fusion = (f32[]{:T(128)}, f32[32,32,128]{2,1,0:T(8,128)S(1)}) fusion(f32[32,32,1]{2,1,0:T(8,128)S(1)} %slice_multiply_fusion, s32[128]{0:T(128)S(1)} %get-tuple-element.34, s32[128]{0:T(128)S(1)} %broadcast_add_fusion.9, s32[128]{0:T(128)S(1)} %get-tuple-element.33, f32[32,32,257]{2,1,0:T(8,128)S(1)} %fusion.10), kind=kOutput, calls=%fused_computation.49 | convolution fusion | flops 403243008 | bytes 2098692 | tf_op jit(solution)/shard_map/dot_general | solution.py:29
  35.9 4.3 %collective-permute-start.3 = (f32[1,32,128]{2,1,0:T(8,128)S(1)}, f32[1,32,128]{2,1,0:T(8,128)S(1)}, u32[]{:S(2)}, u32[]{:S(2)}) collective-permute-start(f32[1,32,128]{2,1,0:T(8,128)S(1)} %slice.357), channel_id=1, source_target_pairs={{0,8},{8,16},{16,24},{1,9},{9,17},{17,25},{2,10},{10,18},{18,26},{... | collective-permute-start | bytes 49160 | tf_op jit(solution)/shard_map/ppermute | solution.py:15
  40.1 1.4 collective-permute-done.3
  41.6 1.3 collective-permute-start.4
  42.9 0.8 collective-permute-done.4
  44.3 4.4 %collective-permute-start.5 = (f32[33,33,1]{1,2,0:T(1,128)S(1)}, f32[33,33,1]{1,2,0:T(1,128)S(1)}, u32[]{:S(2)}, u32[]{:S(2)}) collective-permute-start(f32[33,33,1]{1,2,0:T(1,128)S(1)} %copy.58), channel_id=1, source_target_pairs={{0,1},{1,2},{2,3},{4,5},{5,6},{6,7},{8,9},{9,10},{10,11},{12,13},{... | collective-permute-start | bytes 13076 | tf_op jit(solution)/shard_map/ppermute | solution.py:15
  48.7 1.2 collective-permute-done.5
  52.1 0.9 multiply_reduce_fusion.1
  53.0 4.3 %collective-permute-start.6 = (f32[1,16,64]{2,1,0:T(8,128)S(1)}, f32[1,16,64]{2,1,0:T(8,128)S(1)}, u32[]{:S(2)}, u32[]{:S(2)}) collective-permute-start(f32[1,16,64]{2,1,0:T(8,128)S(1)} %slice.369), channel_id=1, source_target_pairs={{0,8},{8,16},{16,24},{1,9},{9,17},{17,25},{2,10},{10,18},{18,26},{... | collective-permute-start | bytes 12296 | tf_op jit(solution)/shard_map/ppermute | solution.py:15
  57.3 1.3 collective-permute-done.6
  58.7 1.3 collective-permute-start.7
  60.0 0.8 collective-permute-done.7
  60.9 4.2 %collective-permute-start.8 = (f32[17,17,1]{2,1,0:T(8,128)S(1)}, f32[17,17,1]{2,1,0:T(8,128)S(1)}, u32[]{:S(2)}, u32[]{:S(2)}) collective-permute-start(f32[17,17,1]{2,1,0:T(8,128)S(1)} %pad_maximum_fusion.3), channel_id=1, source_target_pairs={{0,1},{1,2},{2,3},{4,5},{5,6},{6,7},{8,9},{9,10},{10,11},{12,13},{... | collective-permute-start | bytes 3476 | tf_op jit(solution)/shard_map/ppermute | solution.py:15
  65.1 4.9 %collective-permute-done.8 = f32[17,17,1]{2,1,0:T(8,128)S(1)} collective-permute-done((f32[17,17,1]{2,1,0:T(8,128)S(1)}, f32[17,17,1]{2,1,0:T(8,128)S(1)}, u32[]{:S(2)}, u32[]{:S(2)}) %collective-permute-start.8) | collective-permute-done | bytes 1188 | tf_op jit(solution)/shard_map/ppermute | solution.py:15
  70.5 0.8 multiply_reduce_fusion.2
  71.3 5.1 %collective-permute-start.9 = (f32[1,8,32]{2,1,0:T(8,128)S(1)}, f32[1,8,32]{2,1,0:T(8,128)S(1)}, u32[]{:S(2)}, u32[]{:S(2)}) collective-permute-start(f32[1,8,32]{2,1,0:T(8,128)S(1)} %slice.381), channel_id=1, source_target_pairs={{0,8},{8,16},{16,24},{1,9},{9,17},{17,25},{2,10},{10,18},{18,26},{... | collective-permute-start | bytes 3080 | tf_op jit(solution)/shard_map/ppermute | solution.py:15
  76.4 1.3 collective-permute-done.9
  77.7 1.3 collective-permute-start.10
  79.0 0.8 collective-permute-done.10
  79.9 4.4 %collective-permute-start.11 = (f32[9,9,1]{2,1,0:T(8,128)S(1)}, f32[9,9,1]{2,1,0:T(8,128)S(1)}, u32[]{:S(2)}, u32[]{:S(2)}) collective-permute-start(f32[9,9,1]{2,1,0:T(8,128)S(1)} %pad_maximum_fusion.5), channel_id=1, source_target_pairs={{0,1},{1,2},{2,3},{4,5},{5,6},{6,7},{8,9},{9,10},{10,11},{12,13},{... | collective-permute-start | bytes 980 | tf_op jit(solution)/shard_map/ppermute | solution.py:15
  84.3 2.0 %collective-permute-done.11 = f32[9,9,1]{2,1,0:T(8,128)S(1)} collective-permute-done((f32[9,9,1]{2,1,0:T(8,128)S(1)}, f32[9,9,1]{2,1,0:T(8,128)S(1)}, u32[]{:S(2)}, u32[]{:S(2)}) %collective-permute-start.11) | collective-permute-done | bytes 356 | tf_op jit(solution)/shard_map/ppermute | solution.py:15
  86.6 0.8 multiply_reduce_fusion.3
  87.5 5.1 %collective-permute-start.12 = (f32[1,4,16]{2,1,0:T(4,128)S(1)}, f32[1,4,16]{2,1,0:T(4,128)S(1)}, u32[]{:S(2)}, u32[]{:S(2)}) collective-permute-start(f32[1,4,16]{2,1,0:T(4,128)S(1)} %slice.393), channel_id=1, source_target_pairs={{0,8},{8,16},{16,24},{1,9},{9,17},{17,25},{2,10},{10,18},{18,26},{... | collective-permute-start | bytes 776 | tf_op jit(solution)/shard_map/ppermute | solution.py:15
  92.5 1.3 collective-permute-done.12
  93.8 1.3 collective-permute-start.13
  95.1 0.8 collective-permute-done.13
  96.0 4.4 %collective-permute-start.14 = (f32[5,5,1]{2,1,0:T(8,128)S(1)}, f32[5,5,1]{2,1,0:T(8,128)S(1)}, u32[]{:S(2)}, u32[]{:S(2)}) collective-permute-start(f32[5,5,1]{2,1,0:T(8,128)S(1)} %pad_maximum_fusion.7), channel_id=1, source_target_pairs={{0,1},{1,2},{2,3},{4,5},{5,6},{6,7},{8,9},{9,10},{10,11},{12,13},{... | collective-permute-start | bytes 308 | tf_op jit(solution)/shard_map/ppermute | solution.py:15
  100.4 1.5 collective-permute-done.14
  102.1 0.8 multiply_reduce_fusion.4
  103.0 3.3 %stack.39 = f32[5]{0:T(128)S(1)} concatenate(f32[1]{0:T(128)} %bitcast.7, f32[1]{0:T(128)} %bitcast.15, f32[1]{0:T(128)} %bitcast.23, f32[1]{0:T(128)} %bitcast.31, f32[1]{0:T(128)} %bitcast.39), dimensions={0} | concatenate | bytes 40 | tf_op jit(solution)/shard_map/stack | solution.py:79
  106.3 43.1 %psum.7 = f32[5]{0:T(128)S(1)} all-reduce(f32[5]{0:T(128)S(1)} %stack.39), channel_id=1, replica_groups=mesh['gx'=4,'gy'=2,'gz'=4] {'gx','gy','gz'}, use_global_device_ids=true, to_apply=%region_5.6 | all-reduce | flops 5 | bytes 40 | tf_op jit(solution)/shard_map/psum | solution.py:79
  153.4 0.9 broadcast_divide_fusion
  (89 shorter events, 9.1 us)
Async XLA Ops:
  1.5 6.8 %collective-permute-start = (f32[1,64,256]{2,1,0:T(8,128)S(1)}, f32[1,64,256]{2,1,0:T(8,128)S(1)}, u32[]{:S(2)}, u32[]{:S(2)}) collective-permute-start(f32[1,64,256]{2,1,0:T(8,128)S(1)} %slice.260), channel_id=1, source_target_pairs={{0,8},{8,16},{16,24},{1,9},{9,17},{17,25},{2,10},{10,18},{18,26},{... | collective-permute-start | bytes 196616 | tf_op jit(solution)/shard_map/ppermute | solution.py:15
  11.2 2.3 %copy-start = (f32[65,64,256]{2,1,0:T(8,128)}, f32[65,64,256]{2,1,0:T(8,128)S(1)}, u32[]{:S(2)}) copy-start(f32[65,64,256]{2,1,0:T(8,128)S(1)} %constant_dynamic-update-slice_fusion) | copy-start | bytes 12779524
  11.3 2.2 %collective-permute-start.1 = (f32[65,1,256]{2,1,0:T(1,128)S(1)}, f32[65,1,256]{2,1,0:T(1,128)S(1)}, u32[]{:S(2)}, u32[]{:S(2)}) collective-permute-start(f32[65,1,256]{2,1,0:T(1,128)S(1)} %slice.345), channel_id=1, source_target_pairs={{0,4},{1,5},{2,6},{3,7},{8,12},{9,13},{10,14},{11,15},{16,20},{17,... | collective-permute-start | bytes 199688 | tf_op jit(solution)/shard_map/ppermute | solution.py:15
  15.1 5.1 %collective-permute-start.2 = (f32[65,65,1]{1,2,0:T(1,128)S(1)}, f32[65,65,1]{1,2,0:T(1,128)S(1)}, u32[]{:S(2)}, u32[]{:S(2)}) collective-permute-start(f32[65,65,1]{1,2,0:T(1,128)S(1)} %copy.49), channel_id=1, source_target_pairs={{0,1},{1,2},{2,3},{4,5},{5,6},{6,7},{8,9},{9,10},{10,11},{12,13},{... | collective-permute-start | bytes 50708 | tf_op jit(solution)/shard_map/ppermute | solution.py:15
  21.1 5.4 %slice-start = ((s8[4259840]{0:T(1024)(128)(4,1)}), s8[4194304]{0:T(1024)(128)(4,1)S(1)}, s32[]{:S(2)}) async-start(s8[4259840]{0:T(1024)(128)(4,1)} %bitcast.208), calls=%async_computation | async-start | bytes 8388608
  25.8 0.8 slice-start.1
  35.9 5.7 %collective-permute-start.3 = (f32[1,32,128]{2,1,0:T(8,128)S(1)}, f32[1,32,128]{2,1,0:T(8,128)S(1)}, u32[]{:S(2)}, u32[]{:S(2)}) collective-permute-start(f32[1,32,128]{2,1,0:T(8,128)S(1)} %slice.357), channel_id=1, source_target_pairs={{0,8},{8,16},{16,24},{1,9},{9,17},{17,25},{2,10},{10,18},{18,26},{... | collective-permute-start | bytes 49160 | tf_op jit(solution)/shard_map/ppermute | solution.py:15
  41.6 2.1 %collective-permute-start.4 = (f32[33,1,128]{2,1,0:T(1,128)S(1)}, f32[33,1,128]{2,1,0:T(1,128)S(1)}, u32[]{:S(2)}, u32[]{:S(2)}) collective-permute-start(f32[33,1,128]{2,1,0:T(1,128)S(1)} %pad_maximum_fusion.9), channel_id=1, source_target_pairs={{0,4},{1,5},{2,6},{3,7},{8,12},{9,13},{10,14},{11,15},{16,20},{17,... | collective-permute-start | bytes 50696 | tf_op jit(solution)/shard_map/ppermute | solution.py:15
  44.3 5.7 %collective-permute-start.5 = (f32[33,33,1]{1,2,0:T(1,128)S(1)}, f32[33,33,1]{1,2,0:T(1,128)S(1)}, u32[]{:S(2)}, u32[]{:S(2)}) collective-permute-start(f32[33,33,1]{1,2,0:T(1,128)S(1)} %copy.58), channel_id=1, source_target_pairs={{0,1},{1,2},{2,3},{4,5},{5,6},{6,7},{8,9},{9,10},{10,11},{12,13},{... | collective-permute-start | bytes 13076 | tf_op jit(solution)/shard_map/ppermute | solution.py:15
  53.0 5.6 %collective-permute-start.6 = (f32[1,16,64]{2,1,0:T(8,128)S(1)}, f32[1,16,64]{2,1,0:T(8,128)S(1)}, u32[]{:S(2)}, u32[]{:S(2)}) collective-permute-start(f32[1,16,64]{2,1,0:T(8,128)S(1)} %slice.369), channel_id=1, source_target_pairs={{0,8},{8,16},{16,24},{1,9},{9,17},{17,25},{2,10},{10,18},{18,26},{... | collective-permute-start | bytes 12296 | tf_op jit(solution)/shard_map/ppermute | solution.py:15
  58.7 2.1 %collective-permute-start.7 = (f32[17,1,64]{2,1,0:T(1,128)S(1)}, f32[17,1,64]{2,1,0:T(1,128)S(1)}, u32[]{:S(2)}, u32[]{:S(2)}) collective-permute-start(f32[17,1,64]{2,1,0:T(1,128)S(1)} %pad_maximum_fusion.10), channel_id=1, source_target_pairs={{0,4},{1,5},{2,6},{3,7},{8,12},{9,13},{10,14},{11,15},{16,20},{17,... | collective-permute-start | bytes 13064 | tf_op jit(solution)/shard_map/ppermute | solution.py:15
  60.9 9.1 %collective-permute-start.8 = (f32[17,17,1]{2,1,0:T(8,128)S(1)}, f32[17,17,1]{2,1,0:T(8,128)S(1)}, u32[]{:S(2)}, u32[]{:S(2)}) collective-permute-start(f32[17,17,1]{2,1,0:T(8,128)S(1)} %pad_maximum_fusion.3), channel_id=1, source_target_pairs={{0,1},{1,2},{2,3},{4,5},{5,6},{6,7},{8,9},{9,10},{10,11},{12,13},{... | collective-permute-start | bytes 3476 | tf_op jit(solution)/shard_map/ppermute | solution.py:15
  71.3 6.4 %collective-permute-start.9 = (f32[1,8,32]{2,1,0:T(8,128)S(1)}, f32[1,8,32]{2,1,0:T(8,128)S(1)}, u32[]{:S(2)}, u32[]{:S(2)}) collective-permute-start(f32[1,8,32]{2,1,0:T(8,128)S(1)} %slice.381), channel_id=1, source_target_pairs={{0,8},{8,16},{16,24},{1,9},{9,17},{17,25},{2,10},{10,18},{18,26},{... | collective-permute-start | bytes 3080 | tf_op jit(solution)/shard_map/ppermute | solution.py:15
  77.7 2.1 %collective-permute-start.10 = (f32[9,1,32]{2,1,0:T(1,128)S(1)}, f32[9,1,32]{2,1,0:T(1,128)S(1)}, u32[]{:S(2)}, u32[]{:S(2)}) collective-permute-start(f32[9,1,32]{2,1,0:T(1,128)S(1)} %pad_maximum_fusion.11), channel_id=1, source_target_pairs={{0,4},{1,5},{2,6},{3,7},{8,12},{9,13},{10,14},{11,15},{16,20},{17,... | collective-permute-start | bytes 3464 | tf_op jit(solution)/shard_map/ppermute | solution.py:15
  79.9 6.4 %collective-permute-start.11 = (f32[9,9,1]{2,1,0:T(8,128)S(1)}, f32[9,9,1]{2,1,0:T(8,128)S(1)}, u32[]{:S(2)}, u32[]{:S(2)}) collective-permute-start(f32[9,9,1]{2,1,0:T(8,128)S(1)} %pad_maximum_fusion.5), channel_id=1, source_target_pairs={{0,1},{1,2},{2,3},{4,5},{5,6},{6,7},{8,9},{9,10},{10,11},{12,13},{... | collective-permute-start | bytes 980 | tf_op jit(solution)/shard_map/ppermute | solution.py:15
  87.5 6.4 %collective-permute-start.12 = (f32[1,4,16]{2,1,0:T(4,128)S(1)}, f32[1,4,16]{2,1,0:T(4,128)S(1)}, u32[]{:S(2)}, u32[]{:S(2)}) collective-permute-start(f32[1,4,16]{2,1,0:T(4,128)S(1)} %slice.393), channel_id=1, source_target_pairs={{0,8},{8,16},{16,24},{1,9},{9,17},{17,25},{2,10},{10,18},{18,26},{... | collective-permute-start | bytes 776 | tf_op jit(solution)/shard_map/ppermute | solution.py:15
  93.8 2.1 %collective-permute-start.13 = (f32[5,1,16]{2,1,0:T(1,128)S(1)}, f32[5,1,16]{2,1,0:T(1,128)S(1)}, u32[]{:S(2)}, u32[]{:S(2)}) collective-permute-start(f32[5,1,16]{2,1,0:T(1,128)S(1)} %pad_maximum_fusion.12), channel_id=1, source_target_pairs={{0,4},{1,5},{2,6},{3,7},{8,12},{9,13},{10,14},{11,15},{16,20},{17,... | collective-permute-start | bytes 968 | tf_op jit(solution)/shard_map/ppermute | solution.py:15
  96.0 5.9 %collective-permute-start.14 = (f32[5,5,1]{2,1,0:T(8,128)S(1)}, f32[5,5,1]{2,1,0:T(8,128)S(1)}, u32[]{:S(2)}, u32[]{:S(2)}) collective-permute-start(f32[5,5,1]{2,1,0:T(8,128)S(1)} %pad_maximum_fusion.7), channel_id=1, source_target_pairs={{0,1},{1,2},{2,3},{4,5},{5,6},{6,7},{8,9},{9,10},{10,11},{12,13},{... | collective-permute-start | bytes 308 | tf_op jit(solution)/shard_map/ppermute | solution.py:15
where the time goes:
time: 158 us; the launch traced here: 157 us
  starting transfers between devices  50.9 us (32%)
  blocking collectives  43.1 us (27%)
  waiting for transfers between devices  22.5 us (14%)
  local copies, waits for them, and re-layouts  15.9 us (10%)
  other arithmetic  15.3 us (10%)
  matrix products  5.1 us (3%)
  between operations  4.72 us (3%)
    ppermute x15, starting transfers between devices, shifted(): return lax.ppermute(block, axis, route)  50.9 us
    psum x1, blocking collectives, per_device(): totals = lax.psum(jnp.stack(sums_local), ('gx', 'gy', 'gz'))  43.1 us
    ppermute x15, waiting for transfers between devices, shifted(): return lax.ppermute(block, axis, route)  22.5 us
    concatenate x5, other arithmetic, extend_cube(): return jnp.concatenate([plane_z, values], axis=2)  5.51 us
    dot_general x5, matrix products, pass_axis(): lax.dot_general(values, table, (((2,), (0,)), ((), ())), precision=lax.Pr...  5.1 us
    add x10, other arithmetic, pass_axis(): return 0.5 * even_part + 0.25 * odd_part + 0.25 * earlier  4.91 us
    div x5, other arithmetic, per_device(): grid_list.append(unscaled[step_no] / product)  3.34 us
    another operation x1, local copies, waits for them, and re-layouts, per_device(): totals = lax.psum(jnp.stack(sums_local), ('gx', 'gy', 'gz'))  3.31 us
  transfers between devices with their start and end apart: 15, of which 15 were waited for; matrix products, arithmetic and copies ran while one was open for 0% of the time, Pallas kernels for 0%

commit v1 on v0

v1 whole, which is shorter than its diff:
```python
import functools

import jax
import jax.numpy as jnp
import ml_dtypes
import numpy as np
from jax import lax
from jax.experimental import pallas as pl
from jax.experimental.pallas import tpu as pltpu
from jax.sharding import PartitionSpec as P

LEVELS = 5
EPSILON = 1e-06
LANES = 128
AXES = ("gx", "gy", "gz")
MESH = pl.DeviceIdType.MESH
HOPS = ((1, 0, 0), (0, 1, 0), (1, 1, 0), (0, 0, 1), (1, 0, 1), (0, 1, 1), (1, 1, 1))


def round_up(n, m):
    return -(-n // m) * m


def step_matrix(n_in, n_cells):
    out = np.zeros((n_cells // 2 + 1, n_in))
    for i in range(n_cells // 2 + 1):
        for off, w in ((-1, 0.25), (0, 0.5), (1, 0.25)):
            if 0 <= 2 * i + off < n_in:
                out[i, 2 * i + off] = w
    return out


def composites(cells):
    mats, m, n = [], None, cells // 2
    for _ in range(LEVELS - 1):
        s = step_matrix(n + 1, n)
        m = s if m is None else s @ m
        mats.append(m)
        n //= 2
    return mats


def exact(table):
    out = table.astype(np.float32).astype(ml_dtypes.bfloat16)
    assert (out.astype(np.float64) == table).all()
    return out


class Plan:
    def __init__(self, shape):
        self.nx, self.ny, self.nz = shape
        self.x1, self.y1, self.z1 = (n // 2 for n in shape)
        assert self.z1 == LANES and self.y1 % 8 == 0
        self.xs = [self.nx >> l for l in range(2, LEVELS + 1)]
        self.ys = [self.ny >> l for l in range(2, LEVELS + 1)]
        self.zs = [self.nz >> l for l in range(2, LEVELS + 1)]
        self.pys = [round_up(y, 8) for y in self.ys]
        self.pxs = [round_up(x, 8) for x in self.xs]
        self.base = np.concatenate([[0], np.cumsum([x * p for x, p in zip(self.xs, self.pys)])]).tolist()
        self.own = round_up(self.base[-1], LANES)
        self.xoff = np.concatenate([[0], np.cumsum(self.pys)]).tolist()
        self.yoff = np.concatenate([[0], np.cumsum(self.pxs)]).tolist()
        self.bx = max(self.y1, self.xoff[-1])
        self.by = max(self.x1, self.yoff[-1])
        self.y0 = self.bx
        self.c0 = self.bx + self.by
        assert self.c0 + 8 <= LANES and self.x1 <= LANES
        self.coff = np.concatenate([[0], np.cumsum(self.zs)]).tolist()
        assert self.coff[-1] <= LANES
        self.main = self.x1 * self.y1
        self.rows1 = self.main + LANES
        self.crows = self.own + LANES

    def row1(self, i, j):
        if i < self.x1 and j < self.y1:
            return i * self.y1 + j
        if j < self.y1:
            return self.main + j
        if i < self.x1:
            return self.main + self.y0 + i
        return self.main + self.c0

    def tables(self):
        xm, ym, zm = composites(self.nx), composites(self.ny), composites(self.nz)
        order = np.array([[self.row1(i, j) for j in range(self.y1 + 1)] for i in range(self.x1 + 1)])
        big = np.zeros((self.crows, self.rows1))
        spread = np.zeros((self.own, LANES))
        for l in range(LEVELS - 1):
            nx, ny = self.xs[l], self.ys[l]
            for i in range(nx + 1):
                for j in range(ny + 1):
                    if i < nx and j < ny:
                        r = self.base[l] + i * self.pys[l] + j
                    elif j < ny:
                        r = self.own + self.xoff[l] + j
                    elif i < nx:
                        r = self.own + self.y0 + self.yoff[l] + i
                    else:
                        r = self.own + self.c0 + l
                    big[r, order] = xm[l][i][:, None] * ym[l][j][None, :]
            for j in range(ny):
                spread[self.base[l] + j, self.xoff[l] + j] = 1
            for i in range(nx):
                spread[self.base[l] + i * self.pys[l], self.y0 + self.yoff[l] + i] = 1
            spread[self.base[l], self.c0 + l] = 1
        z_first = step_matrix(self.nz, self.nz)
        kz1 = np.zeros((self.nz, 2 * LANES))
        kz1[:, :LANES] = z_first[:LANES].T
        kz1[:, LANES:] = z_first[LANES][:, None]
        kz = np.zeros((2 * LANES, LANES))
        tails = np.zeros((16, 2 * LANES))
        place = np.zeros((16, 2 * LANES))
        for l in range(LEVELS - 1):
            kz[: LANES + 1, self.coff[l] : self.coff[l + 1]] = zm[l][:-1].T
            tails[l, : LANES + 1] = zm[l][-1]
            place[l, LANES + self.coff[l]] = 1
        tail1 = np.zeros((16, self.nz))
        tail1[LEVELS - 1] = z_first[LANES]
        place[LEVELS - 1, 0] = 1
        return [exact(t) for t in (kz1, kz, tails, tail1, place, spread, big)]


def halves(x):
    hi = x.astype(jnp.bfloat16)
    return hi, (x - hi.astype(jnp.float32)).astype(jnp.bfloat16)


def dot(a, b, dims=((1,), (0,))):
    return lax.dot_general(a, b, (dims, ((), ())), preferred_element_type=jnp.float32)


def gather_kernel(plan, sizes, chunks, *refs):
    p = plan
    v_hbm, *tabs_hbm = refs[:8]
    out1, outc, stats = refs[8:11]
    (vin, planes, spill, uhi, ulo, z, zhi, zlo, dacc) = refs[11:20]
    tabs = refs[20:27]
    sends = refs[27:32]
    recvs = refs[32:37]
    mine, parts, vsem, tsem, ssem, rsem, assem, arsem = refs[37:45]
    kz1, kz, tails, tail1, place, spread, big = tabs
    pos = [lax.axis_index(a) for a in AXES]
    count = sizes[0] * sizes[1] * sizes[2]
    me = (pos[0] * sizes[1] + pos[1]) * sizes[2] + pos[2]

    def coords(r):
        return {
            "gx": r // (sizes[1] * sizes[2]),
            "gy": (r // sizes[2]) % sizes[1],
            "gz": r % sizes[2],
        }

    barrier = pltpu.get_barrier_semaphore()

    @pl.loop(1, count)
    def _(k):
        pl.semaphore_signal(
            barrier, inc=1, device_id=coords(lax.rem(me + k, count)), device_id_type=MESH
        )

    per = p.nx // chunks
    tcopies = [
        pltpu.make_async_copy(tabs_hbm[i], tabs[i], tsem.at[i]) for i in range(7)
    ]
    vcopies = [
        pltpu.make_async_copy(
            v_hbm.at[pl.ds(c * per, per)], vin.at[pl.ds(1 + c * per, per)], vsem.at[c]
        )
        for c in range(chunks)
    ]
    for i in range(6):
        tcopies[i].start()
    for c in vcopies:
        c.start()
    tcopies[6].start()

    half = per // 2
    vin[0] = jnp.zeros((p.ny, p.nz), jnp.float32)
    lanes = lax.broadcasted_iota(jnp.int32, (p.y1, LANES), 1)
    spill[...] = jnp.zeros_like(spill)
    for j in range(half):
        planes[j, :, 0:8, :] = jnp.zeros((2, 8, LANES), jnp.float32)
    dacc[...] = jnp.zeros_like(dacc)
    for i in range(6):
        tcopies[i].wait()

    def fold_y(j):
        cols = []
        for h in range(2):
            even = planes[j, h, pl.ds(8, p.y1, 2), :]
            odd = planes[j, h, pl.ds(9, p.y1, 2), :]
            prev = planes[j, h, pl.ds(7, p.y1, 2), :]
            cols.append(0.5 * even + 0.25 * (odd + prev))
        return jnp.concatenate(cols, axis=1)

    def last_y(j):
        end = 8 + p.ny
        return jnp.concatenate(
            [0.25 * planes[j, h, end - 1 : end, :] for h in range(2)], axis=1
        )

    def put_plane(j, t):
        for h in range(2):
            planes[j, h, 8:, :] = t[:, h * LANES : (h + 1) * LANES]

    for c in range(chunks):
        vcopies[c].wait()

        @pl.loop(0, half)
        def _(j):
            i = c * half + j
            put_plane(j, 0.5 * vin[2 * i + 1] + 0.25 * (vin[2 * i + 2] + vin[2 * i]))
            hi, lo = halves(fold_y(j))
            rows = pl.ds(pl.multiple_of(i * p.y1, p.y1), p.y1)
            uhi[rows, :] = hi
            ulo[rows, :] = lo
            spill[pl.ds(p.y0 + i, 1), :] = last_y(j)

        rows = pl.ds(c * half * p.y1, half * p.y1)
        z[rows, :] = dot(uhi[rows, :], kz1[...]) + dot(ulo[rows, :], kz1[...])

        @pl.loop(0, half)
        def _(j):
            i = c * half + j
            rows = pl.ds(pl.multiple_of(i * p.y1, p.y1), p.y1)
            plane = z[rows, :]
            dacc[...] += jnp.where(lanes == i, plane[:, LANES:], 0.0)
            hi, lo = halves(plane)
            zhi[rows, :] = hi
            zlo[rows, :] = lo

    put_plane(0, 0.25 * vin[p.nx])
    spill[0 : p.y1, :] = fold_y(0)
    spill[p.c0 : p.c0 + 1, :] = last_y(0)
    shi, slo = halves(spill[...])
    zs = dot(shi, kz1[...]) + dot(slo, kz1[...])
    hi, lo = halves(zs)
    zhi[p.main :, :] = hi
    zlo[p.main :, :] = lo
    tail_one = dot(tail1[...], shi, ((1,), (1,))) + dot(tail1[...], slo, ((1,), (1,)))
    tcopies[6].wait()
    b = dot(big[...], zhi[...]) + dot(big[...], zlo[...])
    bhi, blo = halves(b)
    cs = dot(bhi, kz[...]) + dot(blo, kz[...])
    tail_c = dot(tails[...], bhi, ((1,), (1,))) + dot(tails[...], blo, ((1,), (1,)))

    mx, my, mxy, mz, m8 = sends
    mx[0 : p.bx, :] = zs[0 : p.bx, :LANES]
    mx[p.bx :, :] = cs[p.own : p.own + p.bx]
    my[0 : p.by, :] = zs[p.y0 : p.c0, :LANES]
    my[p.by :, :] = cs[p.own + p.y0 : p.own + p.c0]
    mxy[0:8, :] = zs[p.c0 : p.c0 + 8, :LANES]
    mxy[8:16, :] = cs[p.own + p.c0 : p.own + p.c0 + 8]
    mz[0 : p.y1, :] = dacc[...]
    groups = p.own // LANES
    for g in range(groups):
        mz[p.y1 + 8 * g : p.y1 + 8 * g + 8, :] = tail_c[0:8, g * LANES : (g + 1) * LANES]
    m8[...] = tail_one[0:8] + tail_c[0:8, p.own :]

    pl.semaphore_wait(barrier, count - 1)

    rx, ry, rxy, rz, r8 = recvs
    srcs = [mx, my, mxy, mz, m8, m8, m8]
    dsts = [rx, ry, rxy, rz, r8.at[0], r8.at[1], r8.at[2]]
    has_next, has_prev, copies = [], [], []
    for n, hop in enumerate(HOPS):
        ok_n, ok_p = True, True
        target = {}
        for a in range(3):
            if hop[a]:
                ok_n = jnp.logical_and(ok_n, pos[a] < sizes[a] - 1)
                ok_p = jnp.logical_and(ok_p, pos[a] > 0)
                target[AXES[a]] = lax.rem(pos[a] + 1, sizes[a])
            else:
                target[AXES[a]] = pos[a]
        has_next.append(ok_n)
        has_prev.append(ok_p)
        copies.append(
            pltpu.make_async_remote_copy(
                src_ref=srcs[n],
                dst_ref=dsts[n],
                send_sem=ssem.at[n],
                recv_sem=rsem.at[n],
                device_id=target,
                device_id_type=MESH,
            )
        )
    for n in (3, 0, 1, 2, 4, 5, 6):

        @pl.when(has_next[n])
        def _():
            copies[n].start()

    for n in range(7):

        @pl.when(has_prev[n])
        def _():
            copies[n].wait_recv()

        @pl.when(jnp.logical_not(has_prev[n]))
        def _():
            dsts[n][...] = jnp.zeros(dsts[n].shape, jnp.float32)

    lane8 = lax.broadcasted_iota(jnp.int32, (8, LANES), 1)
    g8 = jnp.where(lane8 < p.y0, r8[0], jnp.where(lane8 < p.c0, r8[1], r8[2]))

    def turned(x, where):
        hi, lo = halves(x.T)
        return dot(hi, where) + dot(lo, where)

    f = turned(g8, place[0:8, :])
    xs1 = rx[0 : p.bx, :] + f[0 : p.bx, :LANES]
    ys1 = ry[0 : p.by, :] + f[p.y0 : p.c0, :LANES]
    xy1 = rxy[0:8, :] + f[p.c0 : p.c0 + 8, :LANES]
    pieces = [
        rx[p.bx :, :] + f[0 : p.bx, LANES:],
        ry[p.by :, :] + f[p.y0 : p.c0, LANES:],
        rxy[8:16, :] + f[p.c0 : p.c0 + 8, LANES:],
    ]
    if p.c0 + 8 < LANES:
        pieces.append(jnp.zeros((LANES - p.c0 - 8, LANES), jnp.float32))
    whi, wlo = halves(jnp.concatenate(pieces, axis=0))
    c = cs[0 : p.own] + dot(spread[...], whi) + dot(spread[...], wlo)
    c = c + jnp.concatenate(
        [
            turned(rz[p.y1 + 8 * g : p.y1 + 8 * g + 8, :], place[0:8, LANES:])
            for g in range(groups)
        ],
        axis=0,
    )
    outc[...] = c

    first = lanes == 0
    top = lax.broadcasted_iota(jnp.int32, (p.y1, LANES), 0) == 0
    col = rz[0 : p.y1, :]
    acc = jnp.zeros((p.y1, LANES), jnp.float32)
    for i in range(p.x1):
        shifted = pltpu.roll(col, (LANES - i) % LANES, 1) if i else col
        plane = z[i * p.y1 : (i + 1) * p.y1, :LANES] + jnp.where(first, shifted, 0.0)
        edge = ys1[i : i + 1, :]
        if i == 0:
            plane = plane + xs1[0 : p.y1]
            edge = edge + xy1[0:1, :]
        plane = plane + jnp.where(top, edge, 0.0)
        out1[i] = plane
        acc = acc + plane * plane
    mine[0:1, :] = jnp.sum(acc, axis=0, keepdims=True)
    sq = c * c
    lane1 = lax.broadcasted_iota(jnp.int32, (1, LANES), 1)
    row = jnp.zeros((1, LANES), jnp.float32)
    for l in range(LEVELS - 1):
        total = jnp.sum(sq[p.base[l] : p.base[l + 1]], axis=0, keepdims=True)
        row = jnp.where((lane1 >= p.coff[l]) & (lane1 < p.coff[l + 1]), total, row)
    mine[1:2, :] = row

    def part(k):
        return pltpu.make_async_remote_copy(
            src_ref=mine,
            dst_ref=parts.at[k],
            send_sem=assem.at[k],
            recv_sem=arsem.at[k],
            device_id=coords(lax.rem(me + k, count)),
            device_id_type=MESH,
        )

    @pl.loop(1, count)
    def _(k):
        part(k).start()

    parts[0] = mine[...]

    for n in range(7):

        @pl.when(has_next[n])
        def _():
            copies[n].wait_send()

    @pl.loop(1, count)
    def _(k):
        part(k).wait_recv()

    stats[...] = jnp.sum(parts[...], axis=0)

    @pl.loop(1, count)
    def _(k):
        part(k).wait_send()


def scale_kernel(plan, devices, grid, packed, stats, o1, o2, o3, o4, o5, scales):
    p = plan
    lane1 = lax.broadcasted_iota(jnp.int32, (1, LANES), 1)
    outs = (o1, o2, o3, o4, o5)
    product = jnp.ones((1, 1), jnp.float32)
    for l in range(LEVELS):
        row = stats[0:1, :] if l == 0 else stats[1:2, :]
        if l:
            row = jnp.where(
                (lane1 >= p.coff[l - 1]) & (lane1 < p.coff[l]), row, 0.0
            )
        total = jnp.sum(row, axis=1, keepdims=True)
        cells = devices * (p.nx >> (l + 1)) * (p.ny >> (l + 1)) * (p.nz >> (l + 1))
        scale = jnp.sqrt(total / (product * product) / cells + EPSILON)
        product = product * scale
        scales[l] = scale[0, 0]
        inverse = 1.0 / product
        if l == 0:
            o1[...] = grid[...] * inverse.reshape(1, 1, 1)
            continue
        k = l - 1
        block = packed[p.base[k] : p.base[k + 1], :] * inverse
        if p.coff[k]:
            block = pltpu.roll(block, LANES - p.coff[k], 1)
        block = block.reshape(p.xs[k], p.pys[k], LANES)
        outs[l][...] = block[:, : p.ys[k], : p.zs[k]]


def per_device(sizes, residual_in):
    plan = Plan(residual_in.shape)
    p = plan
    tables = p.tables()
    chunks = 4
    count = sizes[0] * sizes[1] * sizes[2]
    f32, bf16 = jnp.float32, jnp.bfloat16
    messages = [
        (2 * p.bx, LANES),
        (2 * p.by, LANES),
        (16, LANES),
        (p.y1 + 8 * (p.own // LANES), LANES),
    ]
    anywhere = pl.BlockSpec(memory_space=pl.ANY)
    vmem = pl.BlockSpec(memory_space=pltpu.VMEM)
    dma = pltpu.SemaphoreType.DMA
    grid, packed, stats = pl.pallas_call(
        functools.partial(gather_kernel, p, sizes, chunks),
        out_shape=(
            jax.ShapeDtypeStruct((p.x1, p.y1, p.z1), f32),
            jax.ShapeDtypeStruct((p.own, LANES), f32),
            jax.ShapeDtypeStruct((2, LANES), f32),
        ),
        in_specs=[anywhere] * 8,
        out_specs=(vmem, vmem, vmem),
        scratch_shapes=[
            pltpu.VMEM((p.nx + 1, p.ny, p.nz), f32),
            pltpu.VMEM((p.nx // chunks // 2, 2, 8 + p.ny, LANES), f32),
            pltpu.VMEM((LANES, p.nz), f32),
            pltpu.VMEM((p.main, p.nz), bf16),
            pltpu.VMEM((p.main, p.nz), bf16),
            pltpu.VMEM((p.main, 2 * LANES), f32),
            pltpu.VMEM((p.rows1, 2 * LANES), bf16),
            pltpu.VMEM((p.rows1, 2 * LANES), bf16),
            pltpu.VMEM((p.y1, LANES), f32),
        ]
        + [pltpu.VMEM(t.shape, bf16) for t in tables]
        + [pltpu.VMEM(s, f32) for s in messages + [(8, LANES)]]
        + [pltpu.VMEM(s, f32) for s in messages + [(3, 8, LANES)]]
        + [
            pltpu.VMEM((2, LANES), f32),
            pltpu.VMEM((count, 2, LANES), f32),
            dma((chunks,)),
            dma((7,)),
            dma((7,)),
            dma((7,)),
            dma((count,)),
            dma((count,)),
        ],
        compiler_params=pltpu.CompilerParams(collective_id=0, has_side_effects=True),
        name="restrict_exchange",
    )(residual_in, *[jnp.asarray(t) for t in tables])
    shapes = [
        (p.nx >> l, p.ny >> l, p.nz >> l) for l in range(1, LEVELS + 1)
    ]
    return pl.pallas_call(
        functools.partial(scale_kernel, p, count),
        out_shape=tuple(jax.ShapeDtypeStruct(s, f32) for s in shapes)
        + (jax.ShapeDtypeStruct((LEVELS,), f32),),
        in_specs=[vmem] * 3,
        out_specs=(vmem,) * 5 + (pl.BlockSpec(memory_space=pltpu.SMEM),),
        name="scale_levels",
    )(grid, packed, stats)


def solution(mesh):
    sizes = tuple(mesh.shape[a] for a in AXES)
    spec = P(*AXES)
    return jax.shard_map(
        functools.partial(per_device, sizes),
        mesh=mesh,
        in_specs=(spec,),
        out_specs=(spec,) * 5 + (P(),),
        check_vma=False,
    )
```

time: 158 us -> 24.4 us (0.15)
  starting transfers between devices: 50.9 us -> 0 us
  blocking collectives: 43.1 us -> 0 us
  Pallas kernels: 0 us -> 23.6 us
  waiting for transfers between devices: 22.5 us -> 0 us
  local copies, waits for them, and re-layouts: 15.9 us -> 0 us
  other arithmetic: 15.3 us -> 0 us
  matrix products: 5.1 us -> 0 us
  between operations: 4.72 us -> 0.64 us
    ppermute x15 -> x0, starting transfers between devices: 50.9 us -> none  [shifted(): return lax.ppermute(block, axis, route)]
    psum x1 -> x0, blocking collectives: 43.1 us -> none  [per_device(): totals = lax.psum(jnp.stack(sums_local), ('gx', 'gy', 'gz'))]
    pallas_call x0 -> x2, Pallas kernels: none -> 23.6 us  [the longest x1 21.5 us: per_device(): pl.pallas_call(functools.partial(gather_kernel, p, sizes, chunks), out_sh...]
    ppermute x15 -> x0, waiting for transfers between devices: 22.5 us -> none  [shifted(): return lax.ppermute(block, axis, route)]
    concatenate x14 -> x0, other arithmetic: 6.89 us -> none  [the longest x5 5.51 us: extend_cube(): return jnp.concatenate([plane_z, values], axis=2)]
    slice x41 -> x0, local copies, waits for them, and re-layouts: 6.52 us -> none  [the longest x13 2.67 us: combine_cube(): values = pass_axis(values[:, 1:], 1, values[:, :1])]
    dot_general x5 -> x0, matrix products: 5.1 us -> none  [pass_axis(): lax.dot_general(values, table, (((2,), (0,)), ((), ())), precision=lax.Pr...]
    add x15 -> x0, other arithmetic: 4.93 us -> none  [the longest x10 4.91 us: pass_axis(): return 0.5 * even_part + 0.25 * odd_part + 0.25 * earlier]
  transfers between devices with their start and end apart: 15 -> 0, of which waited for: 15 -> 0; matrix products, arithmetic and copies ran while one was open for 0% -> 0% of each run, Pallas kernels for 0% -> 0%
where the time goes in v1:
time: 24.4 us; the launch traced here: 24.3 us
  Pallas kernels  23.6 us (97%)
  between operations  0.64 us (3%)
    pallas_call x1, Pallas kernels, per_device(): pl.pallas_call(functools.partial(gather_kernel, p, sizes, chunks), out_sh...  21.5 us
    pallas_call x1, Pallas kernels, per_device(): pl.pallas_call(functools.partial(scale_kernel, p, count), out_shape=tuple...  2.13 us

profile of v1, /device:TPU:0, one launch (start us, length us, event | category | flops | bytes accessed | tf_op | source)
XLA Modules:
  0.0 24.3 jit_solution(18197073956447747016)
XLA Ops:
  0.6 21.5 %restrict_exchange.1 = (f32[32,32,128]{2,1,0:T(8,128)}, f32[384,128]{1,0:T(8,128)}, f32[2,128]{1,0:T(2,128)}) custom-call(f32[64,64,256]{2,1,0:T(8,128)} %refs_0_.1, bf16[256,256]{1,0:T(8,128)(2,1)} %constant.14.clone.refs_1_, bf16[256,128]{1,0:T(8,128)(2,1)} %constant.15.clone.refs_2_, bf16[16,256]{1,0:T(8,128)(2,1)} %constant.16.clone.refs_3_, ...), custom_call_target="tpu_custom_call" | custom-call | tf_op jit(solution)/shard_map/restrict_exchange/pallas_call | solution.py:433
  22.1 2.1 %scale_levels.1 = (f32[32,32,128]{2,1,0:T(8,128)}, f32[16,16,64]{2,1,0:T(8,128)}, f32[8,8,32]{2,1,0:T(8,128)}, f32[4,4,16]{2,1,0:T(4,128)}, f32[2,2,8]{2,1,0:T(2,128)}, /*index=5*/f32[5]{0:T(128)}) custom-call(f32[32,32,128]{2,1,0:T(8,128)} %get-tuple-element.9.grid, f32[384,128]{1,0:T(8,128)} %get-tuple-element.10.packed, f32[2,128]{1,0:T(2,128)} %get-tuple-element.11.stats), custom_call_target="tpu_custom_call" | custom-call | tf_op jit(solution)/shard_map/scale_levels/pallas_call | solution.py:472

commit v2 on v1

--- a/solution.py
+++ b/solution.py
@@ -117,7 +117,24 @@
         tail1 = np.zeros((16, self.nz))
         tail1[LEVELS - 1] = z_first[LANES]
         place[LEVELS - 1, 0] = 1
-        return [exact(t) for t in (kz1, kz, tails, tail1, place, spread, big)]
+        return self.pack([kz1, kz, tails, tail1, place, spread], big)
+
+    def pack(self, small, big):
+        blocks = -(-self.rows1 // self.nz)
+        rows = [np.zeros((self.crows, self.nz)) for _ in range(blocks)]
+        for n, block in enumerate(rows):
+            part = big[:, n * self.nz : (n + 1) * self.nz]
+            block[:, : part.shape[1]] = part
+        self.places, self.small = [], []
+        at = blocks * self.crows
+        for t in small:
+            block = np.zeros((t.shape[0], self.nz))
+            block[:, : t.shape[1]] = t
+            rows.append(block)
+            self.places.append((at, 0))
+            self.small.append(t.shape)
+            at += t.shape[0]
+        return exact(np.concatenate(rows))
 
 
 def halves(x):
@@ -131,48 +148,70 @@
 
 def gather_kernel(plan, sizes, chunks, *refs):
     p = plan
-    v_hbm, *tabs_hbm = refs[:8]
-    out1, outc, stats = refs[8:11]
-    (vin, planes, spill, uhi, ulo, z, zhi, zlo, dacc) = refs[11:20]
-    tabs = refs[20:27]
-    sends = refs[27:32]
-    recvs = refs[32:37]
-    mine, parts, vsem, tsem, ssem, rsem, assem, arsem = refs[37:45]
+    v_hbm, packed_hbm = refs[:2]
+    out1_hbm, outc_hbm, stats = refs[2:5]
+    (vin, planes, spill, uhi, ulo, z, zhi, zlo, dacc) = refs[5:14]
+    tabs = refs[14:21]
+    sends = refs[21:30]
+    recvs = refs[30:39]
+    mine, parts = refs[39:41]
+    vsem, tsem, bsem, ssem, rsem, asend, arecv = refs[41:48]
+    out1, outc, osem = refs[48:51]
     kz1, kz, tails, tail1, place, spread, big = tabs
     pos = [lax.axis_index(a) for a in AXES]
-    count = sizes[0] * sizes[1] * sizes[2]
-    me = (pos[0] * sizes[1] + pos[1]) * sizes[2] + pos[2]
-
-    def coords(r):
-        return {
-            "gx": r // (sizes[1] * sizes[2]),
-            "gy": (r // sizes[2]) % sizes[1],
-            "gz": r % sizes[2],
-        }
-
-    barrier = pltpu.get_barrier_semaphore()
-
-    @pl.loop(1, count)
-    def _(k):
-        pl.semaphore_signal(
-            barrier, inc=1, device_id=coords(lax.rem(me + k, count)), device_id_type=MESH
-        )
+    group = sizes[0] * sizes[1]
+    me = pos[0] * sizes[1] + pos[1]
+
+    in_plane = []
+    for k in range(group):
+        r = lax.rem(me + k, group)
+        in_plane.append((r // sizes[1], lax.rem(r, sizes[1])))
+    in_line = [lax.rem(pos[2] + k, sizes[2]) for k in range(sizes[2])]
+    others = [
+        {"gx": gx, "gy": gy, "gz": gz} for gz in in_line for gx, gy in in_plane
+    ][1:]
+
+    def along(hop, way):
+        ok, target = None, {}
+        for a in range(3):
+            target[AXES[a]] = pos[a]
+            if hop[a]:
+                here = pos[a] < sizes[a] - 1 if way > 0 else pos[a] > 0
+                ok = here if ok is None else jnp.logical_and(ok, here)
+                target[AXES[a]] = lax.rem(pos[a] + way + sizes[a], sizes[a])
+        return ok, target
 
     per = p.nx // chunks
     tcopies = [
-        pltpu.make_async_copy(tabs_hbm[i], tabs[i], tsem.at[i]) for i in range(7)
+        pltpu.make_async_copy(
+            packed_hbm.at[pl.ds(at, t.shape[0]), pl.ds(lane, t.shape[1])], t, tsem.at[n]
+        )
+        for n, (t, (at, lane)) in enumerate(zip(tabs[:6], p.places))
     ]
+    blocks = -(-p.rows1 // p.nz)
+    bcopies = []
+    for n in range(blocks):
+        width = min(p.nz, p.rows1 - n * p.nz)
+        bcopies.append(
+            pltpu.make_async_copy(
+                packed_hbm.at[pl.ds(n * p.crows, p.crows), pl.ds(0, width)],
+                big.at[:, pl.ds(n * p.nz, width)],
+                bsem.at[n],
+            )
+        )
     vcopies = [
         pltpu.make_async_copy(
             v_hbm.at[pl.ds(c * per, per)], vin.at[pl.ds(1 + c * per, per)], vsem.at[c]
         )
         for c in range(chunks)
     ]
-    for i in range(6):
-        tcopies[i].start()
-    for c in vcopies:
+    vcopies[0].start()
+    for c in tcopies + vcopies[1:] + bcopies:
         c.start()
-    tcopies[6].start()
+
+    barrier = pltpu.get_barrier_semaphore()
+    for target in others:
+        pl.semaphore_signal(barrier, inc=1, device_id=target, device_id_type=MESH)
 
     half = per // 2
     vin[0] = jnp.zeros((p.ny, p.nz), jnp.float32)
@@ -238,43 +277,22 @@
     zhi[p.main :, :] = hi
     zlo[p.main :, :] = lo
     tail_one = dot(tail1[...], shi, ((1,), (1,))) + dot(tail1[...], slo, ((1,), (1,)))
-    tcopies[6].wait()
-    b = dot(big[...], zhi[...]) + dot(big[...], zlo[...])
-    bhi, blo = halves(b)
-    cs = dot(bhi, kz[...]) + dot(blo, kz[...])
-    tail_c = dot(tails[...], bhi, ((1,), (1,))) + dot(tails[...], blo, ((1,), (1,)))
-
-    mx, my, mxy, mz, m8 = sends
-    mx[0 : p.bx, :] = zs[0 : p.bx, :LANES]
-    mx[p.bx :, :] = cs[p.own : p.own + p.bx]
-    my[0 : p.by, :] = zs[p.y0 : p.c0, :LANES]
-    my[p.by :, :] = cs[p.own + p.y0 : p.own + p.c0]
-    mxy[0:8, :] = zs[p.c0 : p.c0 + 8, :LANES]
-    mxy[8:16, :] = cs[p.own + p.c0 : p.own + p.c0 + 8]
-    mz[0 : p.y1, :] = dacc[...]
-    groups = p.own // LANES
-    for g in range(groups):
-        mz[p.y1 + 8 * g : p.y1 + 8 * g + 8, :] = tail_c[0:8, g * LANES : (g + 1) * LANES]
-    m8[...] = tail_one[0:8] + tail_c[0:8, p.own :]
-
-    pl.semaphore_wait(barrier, count - 1)
-
-    rx, ry, rxy, rz, r8 = recvs
-    srcs = [mx, my, mxy, mz, m8, m8, m8]
-    dsts = [rx, ry, rxy, rz, r8.at[0], r8.at[1], r8.at[2]]
+    mx1, my1, mxy1, mz1, mxc, myc, mxyc, mzc, m8 = sends
+    mx1[...] = zs[0 : p.bx, :LANES]
+    my1[...] = zs[p.y0 : p.c0, :LANES]
+    mxy1[...] = zs[p.c0 : p.c0 + 8, :LANES]
+    mz1[...] = dacc[...]
+    pl.semaphore_wait(barrier, len(others))
+
+    rx1, ry1, rxy1, rz1, rxc, ryc, rxyc, rzc, r8 = recvs
+    srcs = [mx1, my1, mxy1, mz1, mxc, myc, mxyc, mzc, m8, m8, m8]
+    dsts = [rx1, ry1, rxy1, rz1, rxc, ryc, rxyc, rzc, r8.at[0], r8.at[1], r8.at[2]]
+    hops = HOPS[:4] + HOPS[:4] + HOPS[4:]
     has_next, has_prev, copies = [], [], []
-    for n, hop in enumerate(HOPS):
-        ok_n, ok_p = True, True
-        target = {}
-        for a in range(3):
-            if hop[a]:
-                ok_n = jnp.logical_and(ok_n, pos[a] < sizes[a] - 1)
-                ok_p = jnp.logical_and(ok_p, pos[a] > 0)
-                target[AXES[a]] = lax.rem(pos[a] + 1, sizes[a])
-            else:
-                target[AXES[a]] = pos[a]
+    for n, hop in enumerate(hops):
+        ok_n, target = along(hop, 1)
         has_next.append(ok_n)
-        has_prev.append(ok_p)
+        has_prev.append(along(hop, -1)[0])
         copies.append(
             pltpu.make_async_remote_copy(
                 src_ref=srcs[n],
@@ -285,22 +303,43 @@
                 device_id_type=MESH,
             )
         )
-    for n in (3, 0, 1, 2, 4, 5, 6):
-
-        @pl.when(has_next[n])
+
+    def send(which):
+        for n in which:
+
+            @pl.when(has_next[n])
+            def _():
+                copies[n].start()
+
+    send((0, 3, 1, 2))
+    for n in range(len(hops)):
+
+        @pl.when(jnp.logical_not(has_prev[n]))
         def _():
-            copies[n].start()
-
-    for n in range(7):
+            dsts[n][...] = jnp.zeros(dsts[n].shape, jnp.float32)
+
+    for c in bcopies:
+        c.wait()
+    b = dot(big[...], zhi[...]) + dot(big[...], zlo[...])
+    bhi, blo = halves(b)
+    cs = dot(bhi, kz[...]) + dot(blo, kz[...])
+    tail_c = dot(tails[...], bhi, ((1,), (1,))) + dot(tails[...], blo, ((1,), (1,)))
+
+    mxc[...] = cs[p.own : p.own + p.bx]
+    myc[...] = cs[p.own + p.y0 : p.own + p.c0]
+    mxyc[...] = cs[p.own + p.c0 : p.own + p.c0 + 8]
+    groups = p.own // LANES
+    for g in range(groups):
+        mzc[8 * g : 8 * g + 8, :] = tail_c[0:8, g * LANES : (g + 1) * LANES]
+    m8[...] = tail_one[0:8] + tail_c[0:8, p.own :]
+    send((10, 8, 4, 7, 9, 5, 6))
+
+    for n in range(len(hops)):
 
         @pl.when(has_prev[n])
         def _():
             copies[n].wait_recv()
 
-        @pl.when(jnp.logical_not(has_prev[n]))
-        def _():
-            dsts[n][...] = jnp.zeros(dsts[n].shape, jnp.float32)
-
     lane8 = lax.broadcasted_iota(jnp.int32, (8, LANES), 1)
     g8 = jnp.where(lane8 < p.y0, r8[0], jnp.where(lane8 < p.c0, r8[1], r8[2]))
 
@@ -309,13 +348,13 @@
         return dot(hi, where) + dot(lo, where)
 
     f = turned(g8, place[0:8, :])
-    xs1 = rx[0 : p.bx, :] + f[0 : p.bx, :LANES]
-    ys1 = ry[0 : p.by, :] + f[p.y0 : p.c0, :LANES]
-    xy1 = rxy[0:8, :] + f[p.c0 : p.c0 + 8, :LANES]
+    xs1 = rx1[...] + f[0 : p.bx, :LANES]
+    ys1 = ry1[...] + f[p.y0 : p.c0, :LANES]
+    xy1 = rxy1[...] + f[p.c0 : p.c0 + 8, :LANES]
     pieces = [
-        rx[p.bx :, :] + f[0 : p.bx, LANES:],
-        ry[p.by :, :] + f[p.y0 : p.c0, LANES:],
-        rxy[8:16, :] + f[p.c0 : p.c0 + 8, LANES:],
+        rxc[...] + f[0 : p.bx, LANES:],
+        ryc[...] + f[p.y0 : p.c0, LANES:],
+        rxyc[...] + f[p.c0 : p.c0 + 8, LANES:],
     ]
     if p.c0 + 8 < LANES:
         pieces.append(jnp.zeros((LANES - p.c0 - 8, LANES), jnp.float32))
@@ -323,7 +362,7 @@
     c = cs[0 : p.own] + dot(spread[...], whi) + dot(spread[...], wlo)
     c = c + jnp.concatenate(
         [
-            turned(rz[p.y1 + 8 * g : p.y1 + 8 * g + 8, :], place[0:8, LANES:])
+            turned(rzc[8 * g : 8 * g + 8, :], place[0:8, LANES:])
             for g in range(groups)
         ],
         axis=0,
@@ -332,7 +371,7 @@
 
     first = lanes == 0
     top = lax.broadcasted_iota(jnp.int32, (p.y1, LANES), 0) == 0
-    col = rz[0 : p.y1, :]
+    col = rz1[...]
     acc = jnp.zeros((p.y1, LANES), jnp.float32)
     for i in range(p.x1):
         shifted = pltpu.roll(col, (LANES - i) % LANES, 1) if i else col
@@ -344,6 +383,10 @@
         plane = plane + jnp.where(top, edge, 0.0)
         out1[i] = plane
         acc = acc + plane * plane
+    results = [
+        pltpu.make_async_copy(out1, out1_hbm, osem.at[0]),
+        pltpu.make_async_copy(outc, outc_hbm, osem.at[1]),
+    ]
     mine[0:1, :] = jnp.sum(acc, axis=0, keepdims=True)
     sq = c * c
     lane1 = lax.broadcasted_iota(jnp.int32, (1, LANES), 1)
@@ -353,37 +396,35 @@
         row = jnp.where((lane1 >= p.coff[l]) & (lane1 < p.coff[l + 1]), total, row)
     mine[1:2, :] = row
 
-    def part(k):
-        return pltpu.make_async_remote_copy(
+    for c in results:
+        c.start()
+
+    pending = [
+        pltpu.make_async_remote_copy(
             src_ref=mine,
-            dst_ref=parts.at[k],
-            send_sem=assem.at[k],
-            recv_sem=arsem.at[k],
-            device_id=coords(lax.rem(me + k, count)),
+            dst_ref=parts.at[k + 1],
+            send_sem=asend.at[k],
+            recv_sem=arecv.at[k],
+            device_id=target,
             device_id_type=MESH,
         )
-
-    @pl.loop(1, count)
-    def _(k):
-        part(k).start()
-
+        for k, target in enumerate(others)
+    ]
+    for c in reversed(pending):
+        c.start()
     parts[0] = mine[...]
-
-    for n in range(7):
+    for c in pending:
+        c.wait_recv()
+    stats[...] = jnp.sum(parts[...], axis=0)
+    for c in results:
+        c.wait()
+    for c in pending:
+        c.wait_send()
+    for n in range(len(hops)):
 
         @pl.when(has_next[n])
         def _():
             copies[n].wait_send()
-
-    @pl.loop(1, count)
-    def _(k):
-        part(k).wait_recv()
-
-    stats[...] = jnp.sum(parts[...], axis=0)
-
-    @pl.loop(1, count)
-    def _(k):
-        part(k).wait_send()
 
 
 def scale_kernel(plan, devices, grid, packed, stats, o1, o2, o3, o4, o5, scales):
@@ -417,16 +458,12 @@
 def per_device(sizes, residual_in):
     plan = Plan(residual_in.shape)
     p = plan
-    tables = p.tables()
+    packed_table = p.tables()
     chunks = 4
     count = sizes[0] * sizes[1] * sizes[2]
     f32, bf16 = jnp.float32, jnp.bfloat16
-    messages = [
-        (2 * p.bx, LANES),
-        (2 * p.by, LANES),
-        (16, LANES),
-        (p.y1 + 8 * (p.own // LANES), LANES),
-    ]
+    ends = [(p.bx, LANES), (p.by, LANES), (8, LANES)]
+    messages = ends + [(p.y1, LANES)] + ends + [(8 * (p.own // LANES), LANES)]
     anywhere = pl.BlockSpec(memory_space=pl.ANY)
     vmem = pl.BlockSpec(memory_space=pltpu.VMEM)
     dma = pltpu.SemaphoreType.DMA
@@ -437,8 +474,8 @@
             jax.ShapeDtypeStruct((p.own, LANES), f32),
             jax.ShapeDtypeStruct((2, LANES), f32),
         ),
-        in_specs=[anywhere] * 8,
-        out_specs=(vmem, vmem, vmem),
+        in_specs=[anywhere] * 2,
+        out_specs=(anywhere, anywhere, vmem),
         scratch_shapes=[
             pltpu.VMEM((p.nx + 1, p.ny, p.nz), f32),
             pltpu.VMEM((p.nx // chunks // 2, 2, 8 + p.ny, LANES), f32),
@@ -450,22 +487,26 @@
             pltpu.VMEM((p.rows1, 2 * LANES), bf16),
             pltpu.VMEM((p.y1, LANES), f32),
         ]
-        + [pltpu.VMEM(t.shape, bf16) for t in tables]
+        + [pltpu.VMEM(t, bf16) for t in p.small + [(p.crows, p.rows1)]]
         + [pltpu.VMEM(s, f32) for s in messages + [(8, LANES)]]
         + [pltpu.VMEM(s, f32) for s in messages + [(3, 8, LANES)]]
         + [
             pltpu.VMEM((2, LANES), f32),
             pltpu.VMEM((count, 2, LANES), f32),
             dma((chunks,)),
-            dma((7,)),
-            dma((7,)),
-            dma((7,)),
-            dma((count,)),
-            dma((count,)),
+            dma((6,)),
+            dma((-(-p.rows1 // p.nz),)),
+            dma((11,)),
+            dma((11,)),
+            dma((count - 1,)),
+            dma((count - 1,)),
+            pltpu.VMEM((p.x1, p.y1, p.z1), f32),
+            pltpu.VMEM((p.own, LANES), f32),
+            dma((2,)),
         ],
         compiler_params=pltpu.CompilerParams(collective_id=0, has_side_effects=True),
         name="restrict_exchange",
-    )(residual_in, *[jnp.asarray(t) for t in tables])
+    )(residual_in, jnp.asarray(packed_table))
     shapes = [
         (p.nx >> l, p.ny >> l, p.nz >> l) for l in range(1, LEVELS + 1)
     ]

time: 24.4 us -> 23 us (0.943)
  Pallas kernels: 23.6 us -> 22.2 us
    pallas_call x1, Pallas kernels: 21.5 us -> 20.1 us  [per_device(): pl.pallas_call(functools.partial(gather_kernel, p, sizes, chunks), out_sh...]
where the time goes in v2:
time: 23 us; the launch traced here: 22.9 us
  Pallas kernels  22.2 us (97%)
  between operations  0.64 us (3%)
    pallas_call x1, Pallas kernels, per_device(): pl.pallas_call(functools.partial(gather_kernel, p, sizes, chunks), out_sh...  20.1 us
    pallas_call x1, Pallas kernels, per_device(): pl.pallas_call(functools.partial(scale_kernel, p, count), out_shape=tuple...  2.13 us

profile of v2, /device:TPU:0, one launch (start us, length us, event | category | flops | bytes accessed | tf_op | source)
XLA Modules:
  0.0 22.9 jit_solution(7300576393455790638)
XLA Ops:
  0.6 20.1 %restrict_exchange.1 = (f32[32,32,128]{2,1,0:T(8,128)}, f32[384,128]{1,0:T(8,128)}, f32[2,128]{1,0:T(2,128)}) custom-call(f32[64,64,256]{2,1,0:T(8,128)} %refs_0_.1, bf16[3504,256]{1,0:T(8,128)(2,1)} %constant.2.clone.refs_1_), custom_call_target="tpu_custom_call" | custom-call | tf_op jit(solution)/shard_map/restrict_exchange/pallas_call | solution.py:470
  20.7 2.1 %scale_levels.1 = (f32[32,32,128]{2,1,0:T(8,128)}, f32[16,16,64]{2,1,0:T(8,128)}, f32[8,8,32]{2,1,0:T(8,128)}, f32[4,4,16]{2,1,0:T(4,128)}, f32[2,2,8]{2,1,0:T(2,128)}, /*index=5*/f32[5]{0:T(128)}) custom-call(f32[32,32,128]{2,1,0:T(8,128)} %get-tuple-element.9.grid, f32[384,128]{1,0:T(8,128)} %get-tuple-element.10.packed, f32[2,128]{1,0:T(2,128)} %get-tuple-element.11.stats), custom_call_target="tpu_custom_call" | custom-call | tf_op jit(solution)/shard_map/scale_levels/pallas_call | solution.py:513
